TPU v7x, 32 devices: a whole 2x2x4 slice. The times are simulated.
32 devices in a mesh: gossip: 16 (over z, y, core), mp: 2 (over x).
Axes of the slice: x: 2, y: 2, z: 4, core: 2. Of those that a mesh axis runs over, the one named last changes fastest.
Arguments:
- params: float32 [16, 1024, 4096], P('gossip', None, 'mp'), may hold values from -6 to 6
- public: float32 [16, 1024, 64], P('gossip'), may hold values from -12 to 12
- gradients: bfloat16 [2, 16, 1024, 4096], P(None, 'gossip', None, 'mp'), may hold values from -130 to 130
- projection: float32 [4096, 64], P('mp'), may hold values from -0.09375 to 0.09375
- partners: int32 [2, 16], P(None, 'gossip'), may hold values from 0 to 15, as said below
Outputs:
- params_out: float32 [16, 1024, 4096], P('gossip', None, 'mp')
- public_out: float32 [16, 1024, 64], P('gossip')
- consensus: float32 [2], replicated
- grad_norm: float32 [2], replicated
Inputs may be any that keep to these rules, and one draw needn't show every extreme that they name: Each row is a pairing of the 16 replicas: partners[r, partners[r, i]] = i and partners[r, i] != i.
All inputs are finite; a program needn't handle non-finite values.
Results may differ from a plain program's by a relative error of at most 0.008.
Values may be sent and summed in bfloat16 or wider, within the bound.
A program may use at most 64 MiB of HBM per device.

v0:
```python
import jax
import jax.numpy as jnp
from jax import lax
from jax.sharding import PartitionSpec as P

ROUNDS = 2
step_size = 1.0
clip_limit = 0.5
mixing = 0.4
epsilon = 1e-06


def partner_rows(outgoing, table_row):
    initial = outgoing.shape
    entries = outgoing.size
    replicas = lax.axis_size("gossip")
    pieces = outgoing.reshape(replicas, entries // replicas)
    spread = lax.all_to_all(pieces, "gossip", split_axis=0, concat_axis=0, tiled=True)
    reordered = jnp.take(spread, table_row, axis=0)
    back = lax.all_to_all(reordered, "gossip", split_axis=0, concat_axis=0, tiled=True)
    return back.reshape(initial)


def body(params, public, gradients, projection, partners):
    highest = lax.Precision.HIGHEST
    mp_count = lax.axis_size("mp")
    row_count = params.shape[1]
    total = lax.axis_size("gossip") * row_count * projection.shape[0] * mp_count
    weights = params[0]
    public_state = public[0]
    drift_list = []
    norm_list = []
    whole_table = lax.all_gather(partners, "gossip", axis=1, tiled=True)
    for round_index in range(ROUNDS):
        grad_local = gradients[round_index, 0].astype(jnp.float32)
        local_squares = jnp.sum(grad_local * grad_local)
        squares = lax.psum(local_squares, ("gossip", "mp"))
        norm_value = jnp.sqrt(squares / total + epsilon)
        norm_list.append(norm_value)
        scale = jnp.minimum(1.0, clip_limit / norm_value)
        half = weights - step_size * scale * grad_local
        table_row = whole_table[round_index]
        coef_rows = public_state
        rebuilt = jnp.dot(coef_rows, projection.T, precision=highest)
        summed = lax.psum(jnp.dot(half - rebuilt, projection, precision=highest), "mp")
        sent = (public_state + summed).astype(jnp.bfloat16)
        mate = partner_rows(sent, table_row)
        public_state = sent.astype(jnp.float32)
        drift = jnp.dot(mate.astype(jnp.float32) - public_state, projection.T, precision=highest)
        weights = half + mixing * drift
        local_drift = jnp.sum(drift * drift)
        drift_list.append(lax.psum(local_drift, ("gossip", "mp")) / total)
    return (weights[None], public_state[None], jnp.stack(drift_list), jnp.stack(norm_list))


def solution(mesh):
    return jax.shard_map(
        body,
        mesh=mesh,
        in_specs=(
            P("gossip", None, "mp"),
            P("gossip", None, None),
            P(None, "gossip", None, "mp"),
            P("mp", None),
            P(None, "gossip"),
        ),
        out_specs=(P("gossip", None, "mp"), P("gossip", None, None), P(), P()),
        check_vma=False,
    )
```

profile of v0, /device:TPU:12, one launch (start us, length us, event | category | flops | bytes accessed | tf_op | source)
XLA Modules:
  0.0 274.4 jit_solution(1007616994653139488)
XLA Ops:
  7.2 5.2 %fusion.3 = (f32[]{:T(128)}, f32[]{:T(128)}) fusion(bf16[2,1,1024,2048]{3,2,1,0:T(8,128)(2,1)} %param.9), kind=kLoop, calls=%fused_computation.9 | loop fusion | flops 12582910 | bytes 8388616 | tf_op jit(solution)/shard_map/reduce_sum | solution.py:36
  12.4 41.6 %all-reduce.1 = (f32[]{:T(128)}, f32[]{:T(128)}) all-reduce(f32[]{:T(128)} %get-tuple-element.6, f32[]{:T(128)} %get-tuple-element.5), channel_id=1, replica_groups=mesh['gossip'=16,'mp'=2] {'gossip','mp'}, use_global_device_ids=true, to_apply=%region_1.0 | all-reduce | flops 2 | bytes 16 | tf_op jit(solution)/shard_map/psum | solution.py:37
  54.8 6.7 %fusion.16 = f32[1024,2048]{1,0:T(8,128)S(1)} fusion(f32[2048,64]{0,1:T(8,128)S(1)} %copy-done, f32[1,1024,64]{1,2,0:T(8,128)S(1)} %copy-done.2), kind=kOutput, calls=%fused_computation.29 | convolution fusion | flops 1610612736 | bytes 9175040 | tf_op jit(solution)/shard_map/dot_general | solution.py:44
  61.6 12.9 %fusion.8 = f32[1024,64]{0,1:T(8,128)} fusion(f32[2048,64]{0,1:T(8,128)S(1)} %copy-done, f32[1024,2048]{1,0:T(8,128)S(1)} %fusion.16, f32[1,1024,2048]{2,1,0:T(8,128)} %param.7, f32[]{:T(128)S(6)} %min.6, bf16[2,1,1024,2048]{3,2,1,0:T(8,128)(2,1)} %param.9), kind=kOutput, calls=%fused_computation.17 | convolution fusion | flops 1619001344 | bytes 21757956 | tf_op jit(solution)/shard_map/dot_general | solution.py:45
  75.2 14.1 %all-gather = s32[16,1,2]{2,1,0:T(1,128)S(1)} all-gather(s32[1,1,2]{2,1,0:T(1,128)S(1)} %bitcast.64), channel_id=1, replica_groups=mesh['gossip'=16,'mp'=2] {'gossip'}, dimensions={0}, use_global_device_ids=true | all-gather | bytes 136 | tf_op jit(solution)/shard_map/all_gather | solution.py:33
  89.4 7.5 %all-reduce.5.cloned.1.call-done = f32[1024,64]{0,1:T(8,128)} async-done(((f32[1024,64]{0,1:T(8,128)}), f32[1024,64]{0,1:T(8,128)}) %all-reduce.5.cloned.1.call-update) | async-done | bytes 262160 | tf_op jit(solution)/shard_map/psum | solution.py:45
  96.9 1.0 fusion.18
  97.9 0.2 copy.25
  98.0 0.2 all_to_all.38
  98.2 0.5 broadcast.54
  98.7 1.4 reduce.6
  100.1 0.7 reshape.71
  100.8 6.1 %all-to-all-start = ((bf16[16,2,2048]{2,1,0:T(2,128)(2,1)}), bf16[16,2,2048]{2,1,0:T(2,128)(2,1)S(1)}, u32[]{:S(2)}, u32[]{:S(2)}) async-start(bf16[16,2,2048]{2,1,0:T(2,128)(2,1)} %reshape.71), calls=%async_computation | async-start | bytes 262144 | tf_op jit(solution)/shard_map/all_to_all | solution.py:18
  106.9 4.8 %all-to-all-done = bf16[16,2,2048]{2,1,0:T(2,128)(2,1)S(1)} async-done(((bf16[16,2,2048]{2,1,0:T(2,128)(2,1)}), bf16[16,2,2048]{2,1,0:T(2,128)(2,1)S(1)}, u32[]{:S(2)}, u32[]{:S(2)}) %all-to-all-start) | async-done | bytes 131104 | tf_op jit(solution)/shard_map/all_to_all | solution.py:18
  111.7 0.1 reshape.72
  111.8 0.2 copy.38
  112.0 0.6 gather_fusion
  112.7 0.7 reduce.7
  113.4 0.7 reshape.73
  114.1 6.5 %all-to-all-start.1 = ((bf16[16,2,2048]{2,1,0:T(2,128)(2,1)}), bf16[16,2,2048]{2,1,0:T(2,128)(2,1)S(1)}, u32[]{:S(2)}, u32[]{:S(2)}) async-start(bf16[16,2,2048]{2,1,0:T(2,128)(2,1)} %reshape.73), calls=%async_computation.1 | async-start | bytes 262144 | tf_op jit(solution)/shard_map/all_to_all | solution.py:20
  120.7 5.7 %fusion.20 = f32[1024,2048]{1,0:T(8,128)} fusion(bf16[1024,64]{0,1:T(8,128)(2,1)S(1)} %fusion.18, f32[2048,64]{0,1:T(8,128)S(1)} %copy-done), kind=kOutput, calls=%fused_computation.46 | convolution fusion | flops 1610612736 | bytes 9043968 | tf_op jit(solution)/shard_map/dot_general | solution.py:44
  126.5 0.7 convert_reduce_fusion.1
  127.2 0.2 reshape.41
  127.4 0.2 copy.28
  127.6 14.2 %multiply_reduce_fusion.1 = (f32[]{:T(128)}, f32[1024,2048]{1,0:T(8,128)S(1)}) fusion(bf16[2,1,1024,2048]{3,2,1,0:T(8,128)(2,1)} %param.9, f32[]{:T(128)S(6)} %min.7, f32[]{:T(128)S(6)} %min.6, f32[1,1024,2048]{2,1,0:T(8,128)} %param.7, f32[2048,64]{0,1:T(8,128)S(1)} %copy-done, f32[1024,64]{0,1:T(8,128)S(1)} %copy.28, bf16[1024,64]{0,1:T(8,128)(2,1)S(1)} %fusion.18), kind=kOutput, calls=%fused_computation.13 | convolution fusion | flops 1631715328 | bytes 26083340 | tf_op jit(solution)/shard_map/dot_general | solution.py:49
  141.9 3.4 %copy-done.1 = f32[1024,2048]{1,0:T(8,128)} copy-done((f32[1024,2048]{1,0:T(8,128)}, f32[1024,2048]{1,0:T(8,128)S(1)}, u32[]{:S(2)}) %copy-start.1) | copy-done | bytes 8388632
  145.2 11.4 %fusion.6 = f32[1024,64]{0,1:T(8,128)} fusion(f32[2048,64]{0,1:T(8,128)S(1)} %copy-done, f32[1024,2048]{1,0:T(8,128)S(1)} %get-tuple-element.18, f32[1024,2048]{1,0:T(8,128)} %fusion.20), kind=kOutput, calls=%fused_computation.15 | convolution fusion | flops 1612709888 | bytes 17563648 | tf_op jit(solution)/shard_map/dot_general | solution.py:45
  156.7 23.5 %all-reduce.7.cloned.1.call-done = f32[1024,64]{0,1:T(8,128)} async-done(((f32[1024,64]{0,1:T(8,128)}), f32[1024,64]{0,1:T(8,128)}) %all-reduce.7.cloned.1.call-update) | async-done | bytes 262160 | tf_op jit(solution)/shard_map/psum | solution.py:45
  180.2 1.7 convert_bitcast_fusion
  181.8 0.2 copy.29
  182.0 0.2 all_to_all.39
  182.2 1.4 reduce.8
  183.6 0.7 reshape.75
  184.3 6.1 %all-to-all-start.2 = ((bf16[16,2,2048]{2,1,0:T(2,128)(2,1)}), bf16[16,2,2048]{2,1,0:T(2,128)(2,1)S(1)}, u32[]{:S(2)}, u32[]{:S(2)}) async-start(bf16[16,2,2048]{2,1,0:T(2,128)(2,1)} %reshape.75), calls=%async_computation.2 | async-start | bytes 262144 | tf_op jit(solution)/shard_map/all_to_all | solution.py:18
  190.3 4.8 %all-to-all-done.2 = bf16[16,2,2048]{2,1,0:T(2,128)(2,1)S(1)} async-done(((bf16[16,2,2048]{2,1,0:T(2,128)(2,1)}), bf16[16,2,2048]{2,1,0:T(2,128)(2,1)S(1)}, u32[]{:S(2)}, u32[]{:S(2)}) %all-to-all-start.2) | async-done | bytes 131104 | tf_op jit(solution)/shard_map/all_to_all | solution.py:18
  195.3 0.2 copy.37
  195.4 0.6 gather_fusion.1
  196.1 0.7 reduce.9
  196.8 0.7 reshape.77
  197.5 6.5 %all-to-all-start.3 = ((bf16[16,2,2048]{2,1,0:T(2,128)(2,1)}), bf16[16,2,2048]{2,1,0:T(2,128)(2,1)S(1)}, u32[]{:S(2)}, u32[]{:S(2)}) async-start(bf16[16,2,2048]{2,1,0:T(2,128)(2,1)} %reshape.77), calls=%async_computation.3 | async-start | bytes 262144 | tf_op jit(solution)/shard_map/all_to_all | solution.py:20
  204.1 0.6 pad_maximum_fusion.1
  204.6 4.3 %all-to-all-done.3 = bf16[16,2,2048]{2,1,0:T(2,128)(2,1)S(1)} async-done(((bf16[16,2,2048]{2,1,0:T(2,128)(2,1)}), bf16[16,2,2048]{2,1,0:T(2,128)(2,1)S(1)}, u32[]{:S(2)}, u32[]{:S(2)}) %all-to-all-start.3) | async-done | bytes 131104 | tf_op jit(solution)/shard_map/all_to_all | solution.py:20
  209.0 0.7 convert_reduce_fusion
  209.8 0.2 reshape.42
  210.0 0.2 copy.32
  210.2 13.3 %multiply_reduce_fusion = (f32[]{:T(128)}, f32[1,1024,2048]{2,1,0:T(8,128)}) fusion(f32[1024,2048]{1,0:T(8,128)} %copy-done.1, f32[2048,64]{0,1:T(8,128)S(1)} %copy-done, f32[1024,64]{0,1:T(8,128)S(1)} %copy.32, bf16[1024,64]{0,1:T(8,128)(2,1)S(1)} %get-tuple-element.12), kind=kOutput, calls=%fused_computation.12 | convolution fusion | flops 1619132416 | bytes 17694724 | tf_op jit(solution)/shard_map/dot_general | solution.py:49
  223.5 42.2 %all-reduce = (f32[]{:T(128)}, f32[]{:T(128)}) all-reduce(f32[]{:T(128)} %get-tuple-element.19, f32[]{:T(128)} %get-tuple-element.17), channel_id=1, replica_groups=mesh['gossip'=16,'mp'=2] {'gossip','mp'}, use_global_device_ids=true, to_apply=%region_9.11 | all-reduce | flops 2 | bytes 16 | tf_op jit(solution)/shard_map/psum | solution.py:52
  267.0 0.6 pad_maximum_fusion
  (21 shorter events, 0.8 us)
Async XLA Ops:
  7.2 47.6 %copy-start = (f32[2048,64]{0,1:T(8,128)S(1)}, f32[2048,64]{0,1:T(8,128)}, u32[]{:S(2)}) copy-start(f32[2048,64]{0,1:T(8,128)} %param.10) | copy-start | bytes 1572868
  7.2 47.6 %copy-start.2 = (f32[1,1024,64]{1,2,0:T(8,128)S(1)}, f32[1,1024,64]{1,2,0:T(8,128)}, u32[]{:S(2)}) copy-start(f32[1,1024,64]{1,2,0:T(8,128)} %param.8) | copy-start | bytes 786436
  7.2 89.7 %all-reduce.5.cloned.1.call-start = ((), (), s32[]{:S(2)}) async-start(), calls=%async_computation.4 | async-start | bytes 524288 | tf_op jit(solution)/shard_map/psum | solution.py:45
  61.5 13.6 %copy-start.3 = (s32[2,1]{0,1:T(1,128)S(1)}, s32[2,1]{0,1:T(1,128)}, u32[]{:S(2)}) copy-start(s32[2,1]{0,1:T(1,128)} %param.11) | copy-start | bytes 28
  100.8 10.9 %all-to-all-start = ((bf16[16,2,2048]{2,1,0:T(2,128)(2,1)}), bf16[16,2,2048]{2,1,0:T(2,128)(2,1)S(1)}, u32[]{:S(2)}, u32[]{:S(2)}) async-start(bf16[16,2,2048]{2,1,0:T(2,128)(2,1)} %reshape.71), calls=%async_computation | async-start | bytes 262144 | tf_op jit(solution)/shard_map/all_to_all | solution.py:18
  114.1 12.2 %all-to-all-start.1 = ((bf16[16,2,2048]{2,1,0:T(2,128)(2,1)}), bf16[16,2,2048]{2,1,0:T(2,128)(2,1)S(1)}, u32[]{:S(2)}, u32[]{:S(2)}) async-start(bf16[16,2,2048]{2,1,0:T(2,128)(2,1)} %reshape.73), calls=%async_computation.1 | async-start | bytes 262144 | tf_op jit(solution)/shard_map/all_to_all | solution.py:20
  120.6 59.5 %all-reduce.7.cloned.1.call-start = ((), (), s32[]{:S(2)}) async-start(), calls=%async_computation.5 | async-start | bytes 524288 | tf_op jit(solution)/shard_map/psum | solution.py:45
  141.9 3.4 %copy-start.1 = (f32[1024,2048]{1,0:T(8,128)}, f32[1024,2048]{1,0:T(8,128)S(1)}, u32[]{:S(2)}) copy-start(f32[1024,2048]{1,0:T(8,128)S(1)} %get-tuple-element.18) | copy-start | bytes 25165828
  184.3 10.9 %all-to-all-start.2 = ((bf16[16,2,2048]{2,1,0:T(2,128)(2,1)}), bf16[16,2,2048]{2,1,0:T(2,128)(2,1)S(1)}, u32[]{:S(2)}, u32[]{:S(2)}) async-start(bf16[16,2,2048]{2,1,0:T(2,128)(2,1)} %reshape.75), calls=%async_computation.2 | async-start | bytes 262144 | tf_op jit(solution)/shard_map/all_to_all | solution.py:18
  197.5 11.4 %all-to-all-start.3 = ((bf16[16,2,2048]{2,1,0:T(2,128)(2,1)}), bf16[16,2,2048]{2,1,0:T(2,128)(2,1)S(1)}, u32[]{:S(2)}, u32[]{:S(2)}) async-start(bf16[16,2,2048]{2,1,0:T(2,128)(2,1)} %reshape.77), calls=%async_computation.3 | async-start | bytes 262144 | tf_op jit(solution)/shard_map/all_to_all | solution.py:20
Sparse Core Ops, SparseCore 0:
  74.6 22.2 all-reduce.4
  156.8 23.2 all-reduce.6
where the time goes:
time: 275 us; the launch traced here: 274 us
  blocking collectives  97.9 us (36%)
  matrix products  64.2 us (23%)
  waiting for transfers between devices  44.8 us (16%)
  starting transfers between devices  25.2 us (9%)
  between operations  17.1 us (6%)
  other arithmetic  14.8 us (5%)
  local copies, waits for them, and re-layouts  10.4 us (4%)
    psum x1, blocking collectives, body(): drift_list.append(lax.psum(local_drift, ('gossip', 'mp')) / total)  42.2 us
    psum x1, blocking collectives, body(): squares = lax.psum(local_squares, ('gossip', 'mp'))  41.6 us
    psum x2, waiting for transfers between devices, body(): lax.psum(jnp.dot(half - rebuilt, projection, precision=highest), 'mp')  31 us
    dot_general x2, matrix products, body(): jnp.dot(mate.astype(jnp.float32) - public_state, projection.T, precision=...  27.6 us
    dot_general x2, matrix products, body(): jnp.dot(half - rebuilt, projection, precision=highest)  24.3 us
    all_gather x1, blocking collectives, body(): whole_table = lax.all_gather(partners, 'gossip', axis=1, tiled=True)  14.1 us
    all_to_all x2, starting transfers between devices, partner_rows(): lax.all_to_all(reordered, 'gossip', split_axis=0, concat_axis=0, tiled=True)  13 us
    dot_general x2, matrix products, body(): rebuilt = jnp.dot(coef_rows, projection.T, precision=highest)  12.4 us
  transfers between devices with their start and end apart: 6, of which 5 were waited for; matrix products, arithmetic and copies ran while one was open for 2% of the time, Pallas kernels for 0%

commit v1 on v0

--- a/solution.py
+++ b/solution.py
@@ -42,7 +42,9 @@
         table_row = whole_table[round_index]
         coef_rows = public_state
         rebuilt = jnp.dot(coef_rows, projection.T, precision=highest)
-        summed = lax.psum(jnp.dot(half - rebuilt, projection, precision=highest), "mp")
+        summed = jnp.sum(
+            lax.all_gather(jnp.dot(half - rebuilt, projection, precision=highest), "mp"), axis=0
+        )
         sent = (public_state + summed).astype(jnp.bfloat16)
         mate = partner_rows(sent, table_row)
         public_state = sent.astype(jnp.float32)

time: 275 us -> 246 us (0.89)
  waiting for transfers between devices: 44.8 us -> 8.32 us
  blocking collectives: 97.9 us -> 116 us
  between operations: 17.1 us -> 3.74 us
  matrix products: 64.2 us -> 69.2 us
    psum x2 -> x0, waiting for transfers between devices: 31 us -> none  [body(): lax.psum(jnp.dot(half - rebuilt, projection, precision=highest), 'mp')]
    all_gather x0 -> x2, blocking collectives: none -> 16.3 us  [body(): lax.all_gather(jnp.dot(half - rebuilt, projection, precision=highest), 'mp')]
    all_to_all x2, waiting for transfers between devices: 9.58 us -> 4.22 us  [partner_rows(): lax.all_to_all(pieces, 'gossip', split_axis=0, concat_axis=0, tiled=True)]
    all_to_all x2, starting transfers between devices: 13 us -> 16.3 us  [partner_rows(): lax.all_to_all(reordered, 'gossip', split_axis=0, concat_axis=0, tiled=True)]
    unnamed x18 -> x19, local copies, waits for them, and re-layouts: 7.09 us -> 3.92 us
    dot_general x2, matrix products: 24.3 us -> 27.1 us  [body(): jnp.dot(half - rebuilt, projection, precision=highest)]
    all_to_all x2 -> x0, other arithmetic: 2.75 us -> none  [partner_rows(): lax.all_to_all(pieces, 'gossip', split_axis=0, concat_axis=0, tiled=True)]
  transfers between devices with their start and end apart: 6 -> 4, of which waited for: 5 -> 2; matrix products, arithmetic and copies ran while one was open for 2% -> 3% of each run, Pallas kernels for 0% -> 0%
where the time goes in v1:
time: 246 us; the launch traced here: 245 us
  blocking collectives  116 us (47%)
  matrix products  69.2 us (28%)
  starting transfers between devices  27.4 us (11%)
  other arithmetic  12.5 us (5%)
  local copies, waits for them, and re-layouts  8.39 us (3%)
  waiting for transfers between devices  8.32 us (3%)
  between operations  3.74 us (2%)
    psum x1, blocking collectives, body(): drift_list.append(lax.psum(local_drift, ('gossip', 'mp')) / total)  42.2 us
    psum x1, blocking collectives, body(): squares = lax.psum(local_squares, ('gossip', 'mp'))  41.6 us
    dot_general x2, matrix products, body(): jnp.dot(mate.astype(jnp.float32) - public_state, projection.T, precision=...  27.5 us
    dot_general x2, matrix products, body(): jnp.dot(half - rebuilt, projection, precision=highest)  27.1 us
    all_to_all x2, starting transfers between devices, partner_rows(): lax.all_to_all(reordered, 'gossip', split_axis=0, concat_axis=0, tiled=True)  16.3 us
    all_gather x2, blocking collectives, body(): lax.all_gather(jnp.dot(half - rebuilt, projection, precision=highest), 'mp')  16.3 us
    all_gather x1, blocking collectives, body(): whole_table = lax.all_gather(partners, 'gossip', axis=1, tiled=True)  15.6 us
    dot_general x2, matrix products, body(): rebuilt = jnp.dot(coef_rows, projection.T, precision=highest)  14.6 us
  transfers between devices with their start and end apart: 4, of which 2 were waited for; matrix products, arithmetic and copies ran while one was open for 3% of the time, Pallas kernels for 0%

profile of v1, /device:TPU:12, one launch (start us, length us, event | category | flops | bytes accessed | tf_op | source)
XLA Modules:
  0.0 245.2 jit_solution(8556378105193198797)
XLA Ops:
  0.7 5.2 %fusion.3 = (f32[]{:T(128)}, f32[]{:T(128)}) fusion(bf16[2,1,1024,2048]{3,2,1,0:T(8,128)(2,1)} %param.9), kind=kLoop, calls=%fused_computation.9 | loop fusion | flops 12582910 | bytes 8388616 | tf_op jit(solution)/shard_map/reduce_sum | solution.py:36
  5.9 41.6 %all-reduce.1 = (f32[]{:T(128)}, f32[]{:T(128)}) all-reduce(f32[]{:T(128)} %get-tuple-element.10, f32[]{:T(128)} %get-tuple-element.9), channel_id=1, replica_groups=mesh['gossip'=16,'mp'=2] {'gossip','mp'}, use_global_device_ids=true, to_apply=%region_1.0 | all-reduce | flops 2 | bytes 16 | tf_op jit(solution)/shard_map/psum | solution.py:37
  48.2 0.2 copy.31
  48.4 0.2 squeeze.17
  48.6 9.0 %fusion.17 = f32[1024,2048]{1,0:T(8,128)} fusion(f32[2048,64]{0,1:T(8,128)S(1)} %copy-done, f32[1,1024,64]{1,2,0:T(8,128)S(1)} %copy-done.2), kind=kOutput, calls=%fused_computation.30 | convolution fusion | flops 1610612736 | bytes 9175040 | tf_op jit(solution)/shard_map/dot_general | solution.py:44
  57.6 13.3 %fusion.8 = f32[1024,64]{0,1:T(8,128)S(1)} fusion(f32[2048,64]{0,1:T(8,128)S(1)} %copy-done, f32[1024,2048]{1,0:T(8,128)} %fusion.17, f32[1,1024,2048]{2,1,0:T(8,128)} %param.7, f32[]{:T(128)S(6)} %min.6, bf16[2,1,1024,2048]{3,2,1,0:T(8,128)(2,1)} %param.9), kind=kOutput, calls=%fused_computation.17 | convolution fusion | flops 1619001344 | bytes 21757956 | tf_op jit(solution)/shard_map/dot_general | solution.py:46
  71.0 7.0 %all-gather = f32[2048,64]{0,1:T(8,128)S(1)} all-gather(f32[1024,64]{0,1:T(8,128)S(1)} %fusion.8), channel_id=2, replica_groups=mesh['gossip'=16,'mp'=2] {'mp'}, dimensions={0}, use_global_device_ids=true | all-gather | bytes 786432 | tf_op jit(solution)/shard_map/all_gather | solution.py:46
  78.0 0.4 reshape.108
  78.5 0.6 reduce_sum.63
  79.1 0.2 copy.32
  79.3 0.2 reduce_sum.64
  79.5 0.5 broadcast.54
  80.0 0.6 reduce.6
  80.6 0.7 reshape.122
  81.4 5.0 %all-to-all-start = ((bf16[16,2,2048]{2,1,0:T(2,128)(2,1)}), bf16[16,2,2048]{2,1,0:T(2,128)(2,1)S(1)}, u32[]{:S(2)}, u32[]{:S(2)}) async-start(bf16[16,2,2048]{2,1,0:T(2,128)(2,1)} %reshape.122), calls=%async_computation | async-start | bytes 262144 | tf_op jit(solution)/shard_map/all_to_all | solution.py:18
  86.4 15.6 %all-gather.2 = s32[16,1,2]{2,1,0:T(1,128)S(1)} all-gather(s32[1,1,2]{2,1,0:T(1,128)S(1)} %bitcast.80), channel_id=1, replica_groups=mesh['gossip'=16,'mp'=2] {'gossip'}, dimensions={0}, use_global_device_ids=true | all-gather | bytes 136 | tf_op jit(solution)/shard_map/all_gather | solution.py:33
  103.2 0.6 gather_fusion
  103.9 0.6 reduce.7
  104.5 0.7 reshape.124
  105.2 9.8 %all-to-all-start.1 = ((bf16[16,2,2048]{2,1,0:T(2,128)(2,1)}), bf16[16,2,2048]{2,1,0:T(2,128)(2,1)S(1)}, u32[]{:S(2)}, u32[]{:S(2)}) async-start(bf16[16,2,2048]{2,1,0:T(2,128)(2,1)} %reshape.124), calls=%async_computation.1 | async-start | bytes 262144 | tf_op jit(solution)/shard_map/all_to_all | solution.py:20
  115.0 5.7 %fusion.27 = f32[1024,2048]{1,0:T(8,128)} fusion(bf16[1024,64]{0,1:T(8,128)(2,1)S(1)} %fusion.19, f32[2048,64]{0,1:T(8,128)S(1)} %copy-done), kind=kOutput, calls=%fused_computation.53 | convolution fusion | flops 1610612736 | bytes 9043968 | tf_op jit(solution)/shard_map/dot_general | solution.py:44
  120.8 0.7 convert_reduce_fusion.1
  121.5 0.2 reshape.90
  121.7 0.2 copy.35
  121.9 14.2 %multiply_reduce_fusion.1 = (f32[]{:T(128)}, f32[1024,2048]{1,0:T(8,128)S(1)}) fusion(bf16[2,1,1024,2048]{3,2,1,0:T(8,128)(2,1)} %param.9, f32[]{:T(128)S(6)} %min.7, f32[]{:T(128)S(6)} %min.6, f32[1,1024,2048]{2,1,0:T(8,128)} %param.7, f32[2048,64]{0,1:T(8,128)S(1)} %copy-done, f32[1024,64]{0,1:T(8,128)S(1)} %copy.35, bf16[1024,64]{0,1:T(8,128)(2,1)S(1)} %fusion.19), kind=kOutput, calls=%fused_computation.13 | convolution fusion | flops 1631715328 | bytes 26083340 | tf_op jit(solution)/shard_map/dot_general | solution.py:51
  136.1 13.7 %fusion.6 = f32[1024,64]{0,1:T(8,128)S(1)} fusion(f32[2048,64]{0,1:T(8,128)S(1)} %copy-done, f32[1024,2048]{1,0:T(8,128)S(1)} %get-tuple-element.20, f32[1024,2048]{1,0:T(8,128)} %fusion.27), kind=kOutput, calls=%fused_computation.15 | convolution fusion | flops 1612709888 | bytes 17563648 | tf_op jit(solution)/shard_map/dot_general | solution.py:46
  149.9 9.2 %all-gather.1 = f32[2048,64]{0,1:T(8,128)S(1)} all-gather(f32[1024,64]{0,1:T(8,128)S(1)} %fusion.6), channel_id=3, replica_groups=mesh['gossip'=16,'mp'=2] {'mp'}, dimensions={0}, use_global_device_ids=true | all-gather | bytes 786432 | tf_op jit(solution)/shard_map/all_gather | solution.py:46
  159.1 0.4 reshape.109
  159.5 0.6 reduce_sum.66
  160.2 0.2 copy.36
  160.4 0.2 reduce_sum.67
  160.6 0.6 reduce.8
  161.2 0.7 reshape.126
  161.9 6.1 %all-to-all-start.2 = ((bf16[16,2,2048]{2,1,0:T(2,128)(2,1)}), bf16[16,2,2048]{2,1,0:T(2,128)(2,1)S(1)}, u32[]{:S(2)}, u32[]{:S(2)}) async-start(bf16[16,2,2048]{2,1,0:T(2,128)(2,1)} %reshape.126), calls=%async_computation.2 | async-start | bytes 262144 | tf_op jit(solution)/shard_map/all_to_all | solution.py:18
  168.0 0.6 pad_maximum_fusion.1
  168.6 4.2 %all-to-all-done.2 = bf16[16,2,2048]{2,1,0:T(2,128)(2,1)S(1)} async-done(((bf16[16,2,2048]{2,1,0:T(2,128)(2,1)}), bf16[16,2,2048]{2,1,0:T(2,128)(2,1)S(1)}, u32[]{:S(2)}, u32[]{:S(2)}) %all-to-all-start.2) | async-done | bytes 131104 | tf_op jit(solution)/shard_map/all_to_all | solution.py:18
  173.1 0.6 gather_fusion.1
  173.8 0.6 reduce.9
  174.4 0.7 reshape.128
  175.1 6.5 %all-to-all-start.3 = ((bf16[16,2,2048]{2,1,0:T(2,128)(2,1)}), bf16[16,2,2048]{2,1,0:T(2,128)(2,1)S(1)}, u32[]{:S(2)}, u32[]{:S(2)}) async-start(bf16[16,2,2048]{2,1,0:T(2,128)(2,1)} %reshape.128), calls=%async_computation.3 | async-start | bytes 262144 | tf_op jit(solution)/shard_map/all_to_all | solution.py:20
  181.6 0.7 fusion.23
  182.4 4.1 %all-to-all-done.3 = bf16[16,2,2048]{2,1,0:T(2,128)(2,1)S(1)} async-done(((bf16[16,2,2048]{2,1,0:T(2,128)(2,1)}), bf16[16,2,2048]{2,1,0:T(2,128)(2,1)S(1)}, u32[]{:S(2)}, u32[]{:S(2)}) %all-to-all-start.3) | async-done | bytes 131104 | tf_op jit(solution)/shard_map/all_to_all | solution.py:20
  186.6 0.7 convert_reduce_fusion
  187.3 0.2 reshape.91
  187.6 0.2 copy.39
  187.7 13.3 %multiply_reduce_fusion = (f32[]{:T(128)}, f32[1,1024,2048]{2,1,0:T(8,128)}) fusion(f32[1024,2048]{1,0:T(8,128)} %copy-done.1, f32[2048,64]{0,1:T(8,128)S(1)} %copy-done, f32[1024,64]{0,1:T(8,128)S(1)} %copy.39, f32[1024,64]{0,1:T(8,128)S(1)} %reduce_sum.66, bf16[1024,64]{0,1:T(8,128)(2,1)S(1)} %fusion.19), kind=kOutput, calls=%fused_computation.12 | convolution fusion | flops 1619329024 | bytes 17956868 | tf_op jit(solution)/shard_map/dot_general | solution.py:51
  201.1 42.2 %all-reduce = (f32[]{:T(128)}, f32[]{:T(128)}) all-reduce(f32[]{:T(128)} %get-tuple-element.21, f32[]{:T(128)} %get-tuple-element.19), channel_id=1, replica_groups=mesh['gossip'=16,'mp'=2] {'gossip','mp'}, use_global_device_ids=true, to_apply=%region_9.11 | all-reduce | flops 2 | bytes 16 | tf_op jit(solution)/shard_map/psum | solution.py:54
  244.6 0.6 pad_maximum_fusion
  (25 shorter events, 1.2 us)
Async XLA Ops:
  0.6 48.0 %copy-start = (f32[2048,64]{0,1:T(8,128)S(1)}, f32[2048,64]{0,1:T(8,128)}, u32[]{:S(2)}) copy-start(f32[2048,64]{0,1:T(8,128)} %param.10) | copy-start | bytes 1572868
  0.6 47.5 %copy-start.2 = (f32[1,1024,64]{1,2,0:T(8,128)S(1)}, f32[1,1024,64]{1,2,0:T(8,128)}, u32[]{:S(2)}) copy-start(f32[1,1024,64]{1,2,0:T(8,128)} %param.8) | copy-start | bytes 786436
  57.6 28.8 %copy-start.3 = (s32[2,1]{0,1:T(1,128)S(1)}, s32[2,1]{0,1:T(1,128)}, u32[]{:S(2)}) copy-start(s32[2,1]{0,1:T(1,128)} %param.11) | copy-start | bytes 28
  81.4 21.5 %all-to-all-start = ((bf16[16,2,2048]{2,1,0:T(2,128)(2,1)}), bf16[16,2,2048]{2,1,0:T(2,128)(2,1)S(1)}, u32[]{:S(2)}, u32[]{:S(2)}) async-start(bf16[16,2,2048]{2,1,0:T(2,128)(2,1)} %reshape.122), calls=%async_computation | async-start | bytes 262144 | tf_op jit(solution)/shard_map/all_to_all | solution.py:18
  105.2 15.4 %all-to-all-start.1 = ((bf16[16,2,2048]{2,1,0:T(2,128)(2,1)}), bf16[16,2,2048]{2,1,0:T(2,128)(2,1)S(1)}, u32[]{:S(2)}, u32[]{:S(2)}) async-start(bf16[16,2,2048]{2,1,0:T(2,128)(2,1)} %reshape.124), calls=%async_computation.1 | async-start | bytes 262144 | tf_op jit(solution)/shard_map/all_to_all | solution.py:20
  136.1 13.8 %copy-start.1 = (f32[1024,2048]{1,0:T(8,128)}, f32[1024,2048]{1,0:T(8,128)S(1)}, u32[]{:S(2)}) copy-start(f32[1024,2048]{1,0:T(8,128)S(1)} %get-tuple-element.20) | copy-start | bytes 25165828
  161.9 10.9 %all-to-all-start.2 = ((bf16[16,2,2048]{2,1,0:T(2,128)(2,1)}), bf16[16,2,2048]{2,1,0:T(2,128)(2,1)S(1)}, u32[]{:S(2)}, u32[]{:S(2)}) async-start(bf16[16,2,2048]{2,1,0:T(2,128)(2,1)} %reshape.126), calls=%async_computation.2 | async-start | bytes 262144 | tf_op jit(solution)/shard_map/all_to_all | solution.py:18
  175.1 11.4 %all-to-all-start.3 = ((bf16[16,2,2048]{2,1,0:T(2,128)(2,1)}), bf16[16,2,2048]{2,1,0:T(2,128)(2,1)S(1)}, u32[]{:S(2)}, u32[]{:S(2)}) async-start(bf16[16,2,2048]{2,1,0:T(2,128)(2,1)} %reshape.128), calls=%async_computation.3 | async-start | bytes 262144 | tf_op jit(solution)/shard_map/all_to_all | solution.py:20
